TPU v7x, 8 devices: a whole 2x2x1 slice. The times are simulated.
8 devices in a mesh: dp: 1 (over z), tp: 2 (over y), pp: 4 (over x, core).
Axes of the slice: x: 2, y: 2, z: 1, core: 2. Of those that a mesh axis runs over, the one named last changes fastest.
Arguments:
- x_in: bfloat16 [4, 2, 1024, 2816], P(None, 'dp', 'tp')
- ln1_gain: float32 [4, 2816], P('pp')
- ln1_bias: float32 [4, 2816], P('pp')
- w_q: bfloat16 [4, 2816, 2816], P('pp', None, 'tp')
- b_q: float32 [4, 2816], P('pp', 'tp')
- w_kv: bfloat16 [4, 2816, 256], P('pp')
- b_kv: float32 [4, 256], P('pp')
- w_o: bfloat16 [4, 2816, 2816], P('pp', 'tp')
- b_o: float32 [4, 2816], P('pp')
- ln2_gain: float32 [4, 2816], P('pp')
- ln2_bias: float32 [4, 2816], P('pp')
- w_up: bfloat16 [4, 2816, 11264], P('pp', None, 'tp')
- b_up: float32 [4, 11264], P('pp', 'tp')
- w_down: bfloat16 [4, 11264, 2816], P('pp', 'tp')
- b_down: float32 [4, 2816], P('pp')
Outputs:
- output: bfloat16 [4, 4, 2, 1024, 2816], P('pp', None, 'dp', 'tp')
All inputs are finite; a program needn't handle non-finite values.
Results may differ from a plain program's by a relative error of at most 0.0192473.
Values are sent between devices in bfloat16 or wider.
A program may use at most 1 GiB of HBM per device.

v0:
```python
import jax
import jax.numpy as jnp
from jax import lax
from jax.sharding import PartitionSpec as P

PARAM_SPECS = (P('pp', None), P('pp', None), P('pp', None, 'tp'), P('pp', 'tp'), P('pp', None, None), P('pp', None), P('pp', 'tp', None), P('pp', None), P('pp', None), P('pp', None), P('pp', None, 'tp'), P('pp', 'tp'), P('pp', 'tp', None), P('pp', None))


def layer_norm(values, ln_gain, ln_shift):
    average = jnp.mean(values, axis=-1, keepdims=True)
    centered = values - average
    variance = jnp.mean(jnp.square(centered), axis=-1, keepdims=True)
    return centered * lax.rsqrt(variance + 1e-5) * ln_gain + ln_shift


def stage_layer(x_loc, params, tp_size):
    (ln1_gain, ln1_bias, w_q, b_q, w_kv, b_kv, w_o, b_o, ln2_gain, ln2_bias, w_up, b_up, w_down, b_down) = params
    n_batch = x_loc.shape[0]
    seq_len = x_loc.shape[1] * tp_size
    head_dim = w_kv.shape[1] // 2
    heads_loc = w_q.shape[1] // head_dim
    residual = x_loc.astype(jnp.float32)
    normed = layer_norm(residual, ln1_gain, ln1_bias).astype(jnp.bfloat16)
    normed_all = lax.all_gather(normed, 'tp', axis=1, tiled=True)
    queries = (jnp.einsum('bsd,de->bse', normed_all, w_q, preferred_element_type=jnp.float32) + b_q).astype(jnp.bfloat16)
    queries = queries.reshape(n_batch, seq_len, heads_loc, head_dim)
    key_val = (jnp.einsum('bsd,de->bse', normed_all, w_kv, preferred_element_type=jnp.float32) + b_kv).astype(jnp.bfloat16)
    keys_part = key_val[:, :, :head_dim]
    vals_part = key_val[:, :, head_dim:]
    scores = jnp.einsum('crie,cle->cril', queries, keys_part, preferred_element_type=jnp.float32) * (head_dim ** -0.5)
    positions = jnp.arange(seq_len)
    causal = positions[:, None, None] >= positions[None, None, :]
    attn_probs = jax.nn.softmax(jnp.where(causal, scores, -1e30), axis=-1).astype(jnp.bfloat16)
    context = jnp.einsum('cril,cle->crie', attn_probs, vals_part, preferred_element_type=jnp.float32).astype(jnp.bfloat16)
    context = context.reshape(n_batch, seq_len, heads_loc * head_dim)
    attn_part = jnp.einsum('bse,ed->bsd', context, w_o, preferred_element_type=jnp.float32).astype(jnp.bfloat16)
    attn_sum = lax.psum_scatter(attn_part, 'tp', scatter_dimension=1, tiled=True)
    mid_f32 = (residual + attn_sum.astype(jnp.float32) + b_o).astype(jnp.bfloat16).astype(jnp.float32)
    normed2 = layer_norm(mid_f32, ln2_gain, ln2_bias).astype(jnp.bfloat16)
    normed2_all = lax.all_gather(normed2, 'tp', axis=1, tiled=True)
    up_act = jax.nn.gelu(jnp.einsum('bsd,df->bsf', normed2_all, w_up, preferred_element_type=jnp.float32) + b_up, approximate=True).astype(jnp.bfloat16)
    mlp_part = jnp.einsum('bsf,fd->bsd', up_act, w_down, preferred_element_type=jnp.float32).astype(jnp.bfloat16)
    mlp_sum = lax.psum_scatter(mlp_part, 'tp', scatter_dimension=1, tiled=True)
    return (mid_f32 + mlp_sum.astype(jnp.float32) + b_down).astype(jnp.bfloat16)


def solution(mesh):
    tp_size = mesh.shape['tp']
    pp_size = mesh.shape['pp']
    send_pairs = [(from_stage, from_stage + 1) for from_stage in range(pp_size - 1)]

    def stage_program(x_loc, *weights):
        params = tuple(weight[0] for weight in weights)
        n_micro = x_loc.shape[0]
        seq_loc = x_loc.shape[2]
        stage_idx = lax.axis_index('pp')
        tp_rank = lax.axis_index('tp')

        def pipe_step(step_idx, loop_state):
            received, out_buf = loop_state
            fresh_in = lax.dynamic_index_in_dim(x_loc, jnp.minimum(step_idx, n_micro - 1), axis=0, keepdims=False)
            stage_in = jnp.where(stage_idx == 0, fresh_in, received)
            stage_out = stage_layer(stage_in, params, tp_size)
            out_buf = lax.dynamic_update_index_in_dim(out_buf, stage_out, jnp.maximum(step_idx - (pp_size - 1), 0), axis=0)
            gathered = lax.all_gather(stage_out, 'tp', axis=1, tiled=True)
            handed_on = lax.ppermute(gathered, 'pp', send_pairs)
            own_part = lax.dynamic_slice_in_dim(handed_on, tp_rank * seq_loc, seq_loc, axis=1)
            return own_part, out_buf

        init_state = (jnp.zeros_like(x_loc[0]), jnp.zeros_like(x_loc))
        last_state = lax.fori_loop(0, n_micro + pp_size - 1, pipe_step, init_state)
        out_buf = jnp.where(stage_idx == pp_size - 1, last_state[1], jnp.zeros_like(last_state[1]))
        return out_buf[None]

    return jax.shard_map(stage_program, mesh=mesh, in_specs=(P(None, 'dp', 'tp', None),) + PARAM_SPECS, out_specs=P('pp', None, 'dp', 'tp', None), check_vma=False)
```

profile of v0, /device:TPU:7, one launch (start us, length us, event | category | flops | bytes accessed | tf_op | source)
XLA Modules:
  0.0 8056.8 jit_solution(7499602085791433657)
XLA Ops:
  17.3 8012.8 %while.17 = (s32[]{:T(128)}, bf16[2,512,2816]{2,1,0:T(8,128)(2,1)}, bf16[4,2,512,2816]{3,2,1,0:T(8,128)(2,1)}, pred[]{:T(512)}, bf16[4,2,512,2816]{3,2,1,0:T(8,1...) while((s32[]{:T(128)}, bf16[2,512,2816]{2,1,0:T(8,128)(2,1)}, ...), condition=%wide.region_9.10_spmd, body=%wide.region_0.9_spmd.sunk | while | flops 177544364032 | bytes 916377728 | solution.py:71
  37.4 136.6 %all-gather.4.cloned.1.call-done = bf16[2,1024,2816]{2,1,0:T(8,128)(2,1)} async-done(((bf16[2,512,2816]{2,1,0:T(8,128)(2,1)}), bf16[2,1024,2816]{2,1,0:T(8,128)(2,1)}) %all-gather.4.cloned.1.call-update) | async-done | bytes 11534352 | tf_op jit(solution)/shard_map/while/body/eval_jaxpr/all_gather | solution.py:24
  213.5 44.4 fusion.104
  257.9 34.5 fusion.105
  317.8 129.7 %reduce-scatter.3.cloned.1.call-done = bf16[2,512,2816]{2,1,0:T(8,128)(2,1)} async-done(((bf16[2,1024,2816]{2,1,0:T(8,128)(2,1)}), bf16[2,512,2816]{2,1,0:T(8,128)(2,1)}) %reduce-scatter.3.cloned.1.call-update) | async-done | bytes 5767184 | tf_op jit(solution)/shard_map/while/body/eval_jaxpr/reduce_scatter | solution.py:37
  462.7 137.3 %all-gather.6.cloned.1.call-done = bf16[2,1024,2816]{2,1,0:T(8,128)(2,1)} async-done(((bf16[2,512,2816]{2,1,0:T(8,128)(2,1)}), bf16[2,1024,2816]{2,1,0:T(8,128)(2,1)}) %all-gather.6.cloned.1.call-update) | async-done | bytes 11534352 | tf_op jit(solution)/shard_map/while/body/eval_jaxpr/all_gather | solution.py:40
  600.0 75.2 fusion.108
  675.2 89.6 %fusion.109 = bf16[2,1024,2816]{2,1,0:T(8,128)(2,1)} fusion(bf16[5632,2816]{1,0:T(8,128)(2,1)} %get-tuple-element.729, f32[2,1024,5632]{2,1,0:T(8,128)} %fusion.108, f32[5632]{0:T(1024)S(1)} %reduce.23), kind=kOutput, calls=%fused_computation.51.clone.2 | convolution fusion | flops 65082490880 | bytes 89413632 | tf_op jit(solution)/shard_map/while/body/eval_jaxpr/bsf,fd->bsd/dot_general | solution.py:42
  765.5 129.8 %reduce-scatter.5.cloned.1.call-done = bf16[2,512,2816]{2,1,0:T(8,128)(2,1)} async-done(((bf16[2,1024,2816]{2,1,0:T(8,128)(2,1)}), bf16[2,512,2816]{2,1,0:T(8,128)(2,1)}) %reduce-scatter.5.cloned.1.call-update) | async-done | bytes 5767184 | tf_op jit(solution)/shard_map/while/body/eval_jaxpr/reduce_scatter | solution.py:43
  905.9 137.4 %all-gather.8.cloned.1.call-done = bf16[2,1024,2816]{2,1,0:T(8,128)(2,1)} async-done(((bf16[2,512,2816]{2,1,0:T(8,128)(2,1)}), bf16[2,1024,2816]{2,1,0:T(8,128)(2,1)}) %all-gather.8.cloned.1.call-update) | async-done | bytes 11534352 | tf_op jit(solution)/shard_map/while/body/eval_jaxpr/all_gather | solution.py:65
  1088.6 245.3 %all-gather.4.cloned.1.call-done = bf16[2,1024,2816]{2,1,0:T(8,128)(2,1)} async-done(((bf16[2,512,2816]{2,1,0:T(8,128)(2,1)}), bf16[2,1024,2816]{2,1,0:T(8,128)(2,1)}) %all-gather.4.cloned.1.call-update) | async-done | bytes 11534352 | tf_op jit(solution)/shard_map/while/body/eval_jaxpr/all_gather | solution.py:24
  1373.5 44.6 fusion.104
  1418.1 34.5 fusion.105
  1477.7 129.7 %reduce-scatter.3.cloned.1.call-done = bf16[2,512,2816]{2,1,0:T(8,128)(2,1)} async-done(((bf16[2,1024,2816]{2,1,0:T(8,128)(2,1)}), bf16[2,512,2816]{2,1,0:T(8,128)(2,1)}) %reduce-scatter.3.cloned.1.call-update) | async-done | bytes 5767184 | tf_op jit(solution)/shard_map/while/body/eval_jaxpr/reduce_scatter | solution.py:37
  1622.6 137.3 %all-gather.6.cloned.1.call-done = bf16[2,1024,2816]{2,1,0:T(8,128)(2,1)} async-done(((bf16[2,512,2816]{2,1,0:T(8,128)(2,1)}), bf16[2,1024,2816]{2,1,0:T(8,128)(2,1)}) %all-gather.6.cloned.1.call-update) | async-done | bytes 11534352 | tf_op jit(solution)/shard_map/while/body/eval_jaxpr/all_gather | solution.py:40
  1759.9 75.2 fusion.108
  1835.1 89.6 %fusion.109 = bf16[2,1024,2816]{2,1,0:T(8,128)(2,1)} fusion(bf16[5632,2816]{1,0:T(8,128)(2,1)} %get-tuple-element.729, f32[2,1024,5632]{2,1,0:T(8,128)} %fusion.108, f32[5632]{0:T(1024)S(1)} %reduce.23), kind=kOutput, calls=%fused_computation.51.clone.2 | convolution fusion | flops 65082490880 | bytes 89413632 | tf_op jit(solution)/shard_map/while/body/eval_jaxpr/bsf,fd->bsd/dot_general | solution.py:42
  1925.4 129.8 %reduce-scatter.5.cloned.1.call-done = bf16[2,512,2816]{2,1,0:T(8,128)(2,1)} async-done(((bf16[2,1024,2816]{2,1,0:T(8,128)(2,1)}), bf16[2,512,2816]{2,1,0:T(8,128)(2,1)}) %reduce-scatter.5.cloned.1.call-update) | async-done | bytes 5767184 | tf_op jit(solution)/shard_map/while/body/eval_jaxpr/reduce_scatter | solution.py:43
  2065.8 137.4 %all-gather.8.cloned.1.call-done = bf16[2,1024,2816]{2,1,0:T(8,128)(2,1)} async-done(((bf16[2,512,2816]{2,1,0:T(8,128)(2,1)}), bf16[2,1024,2816]{2,1,0:T(8,128)(2,1)}) %all-gather.8.cloned.1.call-update) | async-done | bytes 11534352 | tf_op jit(solution)/shard_map/while/body/eval_jaxpr/all_gather | solution.py:65
  2248.6 245.4 %all-gather.4.cloned.1.call-done = bf16[2,1024,2816]{2,1,0:T(8,128)(2,1)} async-done(((bf16[2,512,2816]{2,1,0:T(8,128)(2,1)}), bf16[2,1024,2816]{2,1,0:T(8,128)(2,1)}) %all-gather.4.cloned.1.call-update) | async-done | bytes 11534352 | tf_op jit(solution)/shard_map/while/body/eval_jaxpr/all_gather | solution.py:24
  2533.6 44.4 fusion.104
  2578.0 34.5 fusion.105
  2637.9 129.7 %reduce-scatter.3.cloned.1.call-done = bf16[2,512,2816]{2,1,0:T(8,128)(2,1)} async-done(((bf16[2,1024,2816]{2,1,0:T(8,128)(2,1)}), bf16[2,512,2816]{2,1,0:T(8,128)(2,1)}) %reduce-scatter.3.cloned.1.call-update) | async-done | bytes 5767184 | tf_op jit(solution)/shard_map/while/body/eval_jaxpr/reduce_scatter | solution.py:37
  2782.8 137.3 %all-gather.6.cloned.1.call-done = bf16[2,1024,2816]{2,1,0:T(8,128)(2,1)} async-done(((bf16[2,512,2816]{2,1,0:T(8,128)(2,1)}), bf16[2,1024,2816]{2,1,0:T(8,128)(2,1)}) %all-gather.6.cloned.1.call-update) | async-done | bytes 11534352 | tf_op jit(solution)/shard_map/while/body/eval_jaxpr/all_gather | solution.py:40
  2920.0 75.2 fusion.108
  2995.2 89.6 %fusion.109 = bf16[2,1024,2816]{2,1,0:T(8,128)(2,1)} fusion(bf16[5632,2816]{1,0:T(8,128)(2,1)} %get-tuple-element.729, f32[2,1024,5632]{2,1,0:T(8,128)} %fusion.108, f32[5632]{0:T(1024)S(1)} %reduce.23), kind=kOutput, calls=%fused_computation.51.clone.2 | convolution fusion | flops 65082490880 | bytes 89413632 | tf_op jit(solution)/shard_map/while/body/eval_jaxpr/bsf,fd->bsd/dot_general | solution.py:42
  3085.6 129.8 %reduce-scatter.5.cloned.1.call-done = bf16[2,512,2816]{2,1,0:T(8,128)(2,1)} async-done(((bf16[2,1024,2816]{2,1,0:T(8,128)(2,1)}), bf16[2,512,2816]{2,1,0:T(8,128)(2,1)}) %reduce-scatter.5.cloned.1.call-update) | async-done | bytes 5767184 | tf_op jit(solution)/shard_map/while/body/eval_jaxpr/reduce_scatter | solution.py:43
  3226.0 137.4 %all-gather.8.cloned.1.call-done = bf16[2,1024,2816]{2,1,0:T(8,128)(2,1)} async-done(((bf16[2,512,2816]{2,1,0:T(8,128)(2,1)}), bf16[2,1024,2816]{2,1,0:T(8,128)(2,1)}) %all-gather.8.cloned.1.call-update) | async-done | bytes 11534352 | tf_op jit(solution)/shard_map/while/body/eval_jaxpr/all_gather | solution.py:65
  3408.7 245.3 %all-gather.4.cloned.1.call-done = bf16[2,1024,2816]{2,1,0:T(8,128)(2,1)} async-done(((bf16[2,512,2816]{2,1,0:T(8,128)(2,1)}), bf16[2,1024,2816]{2,1,0:T(8,128)(2,1)}) %all-gather.4.cloned.1.call-update) | async-done | bytes 11534352 | tf_op jit(solution)/shard_map/while/body/eval_jaxpr/all_gather | solution.py:24
  3693.5 44.6 fusion.104
  3738.2 34.5 fusion.105
  3797.8 129.7 %reduce-scatter.3.cloned.1.call-done = bf16[2,512,2816]{2,1,0:T(8,128)(2,1)} async-done(((bf16[2,1024,2816]{2,1,0:T(8,128)(2,1)}), bf16[2,512,2816]{2,1,0:T(8,128)(2,1)}) %reduce-scatter.3.cloned.1.call-update) | async-done | bytes 5767184 | tf_op jit(solution)/shard_map/while/body/eval_jaxpr/reduce_scatter | solution.py:37
  3942.7 137.3 %all-gather.6.cloned.1.call-done = bf16[2,1024,2816]{2,1,0:T(8,128)(2,1)} async-done(((bf16[2,512,2816]{2,1,0:T(8,128)(2,1)}), bf16[2,1024,2816]{2,1,0:T(8,128)(2,1)}) %all-gather.6.cloned.1.call-update) | async-done | bytes 11534352 | tf_op jit(solution)/shard_map/while/body/eval_jaxpr/all_gather | solution.py:40
  4079.9 75.2 fusion.108
  4155.1 89.6 %fusion.109 = bf16[2,1024,2816]{2,1,0:T(8,128)(2,1)} fusion(bf16[5632,2816]{1,0:T(8,128)(2,1)} %get-tuple-element.729, f32[2,1024,5632]{2,1,0:T(8,128)} %fusion.108, f32[5632]{0:T(1024)S(1)} %reduce.23), kind=kOutput, calls=%fused_computation.51.clone.2 | convolution fusion | flops 65082490880 | bytes 89413632 | tf_op jit(solution)/shard_map/while/body/eval_jaxpr/bsf,fd->bsd/dot_general | solution.py:42
  4245.5 129.8 %reduce-scatter.5.cloned.1.call-done = bf16[2,512,2816]{2,1,0:T(8,128)(2,1)} async-done(((bf16[2,1024,2816]{2,1,0:T(8,128)(2,1)}), bf16[2,512,2816]{2,1,0:T(8,128)(2,1)}) %reduce-scatter.5.cloned.1.call-update) | async-done | bytes 5767184 | tf_op jit(solution)/shard_map/while/body/eval_jaxpr/reduce_scatter | solution.py:43
  4385.9 137.4 %all-gather.8.cloned.1.call-done = bf16[2,1024,2816]{2,1,0:T(8,128)(2,1)} async-done(((bf16[2,512,2816]{2,1,0:T(8,128)(2,1)}), bf16[2,1024,2816]{2,1,0:T(8,128)(2,1)}) %all-gather.8.cloned.1.call-update) | async-done | bytes 11534352 | tf_op jit(solution)/shard_map/while/body/eval_jaxpr/all_gather | solution.py:65
  4568.7 245.4 %all-gather.4.cloned.1.call-done = bf16[2,1024,2816]{2,1,0:T(8,128)(2,1)} async-done(((bf16[2,512,2816]{2,1,0:T(8,128)(2,1)}), bf16[2,1024,2816]{2,1,0:T(8,128)(2,1)}) %all-gather.4.cloned.1.call-update) | async-done | bytes 11534352 | tf_op jit(solution)/shard_map/while/body/eval_jaxpr/all_gather | solution.py:24
  4853.7 44.4 fusion.104
  4898.1 34.5 fusion.105
  4958.0 129.7 %reduce-scatter.3.cloned.1.call-done = bf16[2,512,2816]{2,1,0:T(8,128)(2,1)} async-done(((bf16[2,1024,2816]{2,1,0:T(8,128)(2,1)}), bf16[2,512,2816]{2,1,0:T(8,128)(2,1)}) %reduce-scatter.3.cloned.1.call-update) | async-done | bytes 5767184 | tf_op jit(solution)/shard_map/while/body/eval_jaxpr/reduce_scatter | solution.py:37
  5102.8 137.3 %all-gather.6.cloned.1.call-done = bf16[2,1024,2816]{2,1,0:T(8,128)(2,1)} async-done(((bf16[2,512,2816]{2,1,0:T(8,128)(2,1)}), bf16[2,1024,2816]{2,1,0:T(8,128)(2,1)}) %all-gather.6.cloned.1.call-update) | async-done | bytes 11534352 | tf_op jit(solution)/shard_map/while/body/eval_jaxpr/all_gather | solution.py:40
  5240.1 75.2 fusion.108
  5315.3 89.6 %fusion.109 = bf16[2,1024,2816]{2,1,0:T(8,128)(2,1)} fusion(bf16[5632,2816]{1,0:T(8,128)(2,1)} %get-tuple-element.729, f32[2,1024,5632]{2,1,0:T(8,128)} %fusion.108, f32[5632]{0:T(1024)S(1)} %reduce.23), kind=kOutput, calls=%fused_computation.51.clone.2 | convolution fusion | flops 65082490880 | bytes 89413632 | tf_op jit(solution)/shard_map/while/body/eval_jaxpr/bsf,fd->bsd/dot_general | solution.py:42
  5405.7 129.8 %reduce-scatter.5.cloned.1.call-done = bf16[2,512,2816]{2,1,0:T(8,128)(2,1)} async-done(((bf16[2,1024,2816]{2,1,0:T(8,128)(2,1)}), bf16[2,512,2816]{2,1,0:T(8,128)(2,1)}) %reduce-scatter.5.cloned.1.call-update) | async-done | bytes 5767184 | tf_op jit(solution)/shard_map/while/body/eval_jaxpr/reduce_scatter | solution.py:43
  5546.0 137.4 %all-gather.8.cloned.1.call-done = bf16[2,1024,2816]{2,1,0:T(8,128)(2,1)} async-done(((bf16[2,512,2816]{2,1,0:T(8,128)(2,1)}), bf16[2,1024,2816]{2,1,0:T(8,128)(2,1)}) %all-gather.8.cloned.1.call-update) | async-done | bytes 11534352 | tf_op jit(solution)/shard_map/while/body/eval_jaxpr/all_gather | solution.py:65
  5728.7 245.3 %all-gather.4.cloned.1.call-done = bf16[2,1024,2816]{2,1,0:T(8,128)(2,1)} async-done(((bf16[2,512,2816]{2,1,0:T(8,128)(2,1)}), bf16[2,1024,2816]{2,1,0:T(8,128)(2,1)}) %all-gather.4.cloned.1.call-update) | async-done | bytes 11534352 | tf_op jit(solution)/shard_map/while/body/eval_jaxpr/all_gather | solution.py:24
  6013.6 44.6 fusion.104
  6058.2 34.5 fusion.105
  6117.9 129.7 %reduce-scatter.3.cloned.1.call-done = bf16[2,512,2816]{2,1,0:T(8,128)(2,1)} async-done(((bf16[2,1024,2816]{2,1,0:T(8,128)(2,1)}), bf16[2,512,2816]{2,1,0:T(8,128)(2,1)}) %reduce-scatter.3.cloned.1.call-update) | async-done | bytes 5767184 | tf_op jit(solution)/shard_map/while/body/eval_jaxpr/reduce_scatter | solution.py:37
  6262.7 137.3 %all-gather.6.cloned.1.call-done = bf16[2,1024,2816]{2,1,0:T(8,128)(2,1)} async-done(((bf16[2,512,2816]{2,1,0:T(8,128)(2,1)}), bf16[2,1024,2816]{2,1,0:T(8,128)(2,1)}) %all-gather.6.cloned.1.call-update) | async-done | bytes 11534352 | tf_op jit(solution)/shard_map/while/body/eval_jaxpr/all_gather | solution.py:40
  6400.0 75.2 fusion.108
  6475.2 89.6 %fusion.109 = bf16[2,1024,2816]{2,1,0:T(8,128)(2,1)} fusion(bf16[5632,2816]{1,0:T(8,128)(2,1)} %get-tuple-element.729, f32[2,1024,5632]{2,1,0:T(8,128)} %fusion.108, f32[5632]{0:T(1024)S(1)} %reduce.23), kind=kOutput, calls=%fused_computation.51.clone.2 | convolution fusion | flops 65082490880 | bytes 89413632 | tf_op jit(solution)/shard_map/while/body/eval_jaxpr/bsf,fd->bsd/dot_general | solution.py:42
  6565.6 129.8 %reduce-scatter.5.cloned.1.call-done = bf16[2,512,2816]{2,1,0:T(8,128)(2,1)} async-done(((bf16[2,1024,2816]{2,1,0:T(8,128)(2,1)}), bf16[2,512,2816]{2,1,0:T(8,128)(2,1)}) %reduce-scatter.5.cloned.1.call-update) | async-done | bytes 5767184 | tf_op jit(solution)/shard_map/while/body/eval_jaxpr/reduce_scatter | solution.py:43
  6706.0 137.4 %all-gather.8.cloned.1.call-done = bf16[2,1024,2816]{2,1,0:T(8,128)(2,1)} async-done(((bf16[2,512,2816]{2,1,0:T(8,128)(2,1)}), bf16[2,1024,2816]{2,1,0:T(8,128)(2,1)}) %all-gather.8.cloned.1.call-update) | async-done | bytes 11534352 | tf_op jit(solution)/shard_map/while/body/eval_jaxpr/all_gather | solution.py:65
  6888.8 245.4 %all-gather.4.cloned.1.call-done = bf16[2,1024,2816]{2,1,0:T(8,128)(2,1)} async-done(((bf16[2,512,2816]{2,1,0:T(8,128)(2,1)}), bf16[2,1024,2816]{2,1,0:T(8,128)(2,1)}) %all-gather.4.cloned.1.call-update) | async-done | bytes 11534352 | tf_op jit(solution)/shard_map/while/body/eval_jaxpr/all_gather | solution.py:24
  7173.7 44.4 fusion.104
  7218.1 34.5 fusion.105
  7278.1 129.7 %reduce-scatter.3.cloned.1.call-done = bf16[2,512,2816]{2,1,0:T(8,128)(2,1)} async-done(((bf16[2,1024,2816]{2,1,0:T(8,128)(2,1)}), bf16[2,512,2816]{2,1,0:T(8,128)(2,1)}) %reduce-scatter.3.cloned.1.call-update) | async-done | bytes 5767184 | tf_op jit(solution)/shard_map/while/body/eval_jaxpr/reduce_scatter | solution.py:37
  7422.9 137.3 %all-gather.6.cloned.1.call-done = bf16[2,1024,2816]{2,1,0:T(8,128)(2,1)} async-done(((bf16[2,512,2816]{2,1,0:T(8,128)(2,1)}), bf16[2,1024,2816]{2,1,0:T(8,128)(2,1)}) %all-gather.6.cloned.1.call-update) | async-done | bytes 11534352 | tf_op jit(solution)/shard_map/while/body/eval_jaxpr/all_gather | solution.py:40
  7560.2 75.2 fusion.108
  7635.4 89.6 %fusion.109 = bf16[2,1024,2816]{2,1,0:T(8,128)(2,1)} fusion(bf16[5632,2816]{1,0:T(8,128)(2,1)} %get-tuple-element.729, f32[2,1024,5632]{2,1,0:T(8,128)} %fusion.108, f32[5632]{0:T(1024)S(1)} %reduce.23), kind=kOutput, calls=%fused_computation.51.clone.2 | convolution fusion | flops 65082490880 | bytes 89413632 | tf_op jit(solution)/shard_map/while/body/eval_jaxpr/bsf,fd->bsd/dot_general | solution.py:42
  7725.7 129.8 %reduce-scatter.5.cloned.1.call-done = bf16[2,512,2816]{2,1,0:T(8,128)(2,1)} async-done(((bf16[2,1024,2816]{2,1,0:T(8,128)(2,1)}), bf16[2,512,2816]{2,1,0:T(8,128)(2,1)}) %reduce-scatter.5.cloned.1.call-update) | async-done | bytes 5767184 | tf_op jit(solution)/shard_map/while/body/eval_jaxpr/reduce_scatter | solution.py:43
  7866.1 137.4 %all-gather.8.cloned.1.call-done = bf16[2,1024,2816]{2,1,0:T(8,128)(2,1)} async-done(((bf16[2,512,2816]{2,1,0:T(8,128)(2,1)}), bf16[2,1024,2816]{2,1,0:T(8,128)(2,1)}) %all-gather.8.cloned.1.call-update) | async-done | bytes 11534352 | tf_op jit(solution)/shard_map/while/body/eval_jaxpr/all_gather | solution.py:65
  (440 shorter events, 983.4 us)
Async XLA Ops:
  17.8 156.2 %all-gather.4.cloned.1.call-start = ((), (), s32[]{:S(2)}) async-start(), calls=%async_computation.2 | async-start | bytes 17301504 | tf_op jit(solution)/shard_map/while/body/eval_jaxpr/all_gather | solution.py:24
  36.8 410.7 %reduce-scatter.3.cloned.1.call-start = ((), (), s32[]{:S(2)}) async-start(), calls=%async_computation.3 | async-start | bytes 17301504 | tf_op jit(solution)/shard_map/while/body/eval_jaxpr/reduce_scatter | solution.py:37
  317.0 282.9 %all-gather.6.cloned.1.call-start = ((), (), s32[]{:S(2)}) async-start(), calls=%async_computation.4 | async-start | bytes 17301504 | tf_op jit(solution)/shard_map/while/body/eval_jaxpr/all_gather | solution.py:40
  462.6 432.7 %reduce-scatter.5.cloned.1.call-start = ((), (), s32[]{:S(2)}) async-start(), calls=%async_computation.5 | async-start | bytes 17301504 | tf_op jit(solution)/shard_map/while/body/eval_jaxpr/reduce_scatter | solution.py:43
  764.8 278.5 %all-gather.8.cloned.1.call-start = ((), (), s32[]{:S(2)}) async-start(), calls=%async_computation.6 | async-start | bytes 17301504 | tf_op jit(solution)/shard_map/while/body/eval_jaxpr/all_gather | solution.py:65
  905.8 162.8 %copy-start.12 = (f32[1,1408]{1,0:T(1,128)S(1)}, f32[1,1408]{1,0:T(1,128)}, u32[]{:S(2)}) copy-start(f32[1,1408]{1,0:T(1,128)} %get-tuple-element.838) | copy-start | bytes 16900 | tf_op jit(solution)/shard_map/while
  905.8 162.8 %copy-start.14 = (bf16[1,2816,256]{2,1,0:T(8,128)(2,1)S(1)}, bf16[1,2816,256]{2,1,0:T(8,128)(2,1)}, u32[]{:S(2)}) copy-start(bf16[1,2816,256]{2,1,0:T(8,128)(2,1)} %get-tuple-element.872) | copy-start | bytes 4325380 | tf_op jit(solution)/shard_map/while
  905.8 162.8 %copy-start.16 = (f32[1,256]{1,0:T(1,128)S(1)}, f32[1,256]{1,0:T(1,128)}, u32[]{:S(2)}) copy-start(f32[1,256]{1,0:T(1,128)} %get-tuple-element.903) | copy-start | bytes 3076 | tf_op jit(solution)/shard_map/while
  1043.3 19.9 collective-permute-start
  1068.9 265.0 %all-gather.4.cloned.1.call-start = ((), (), s32[]{:S(2)}) async-start(), calls=%async_computation.2 | async-start | bytes 17301504 | tf_op jit(solution)/shard_map/while/body/eval_jaxpr/all_gather | solution.py:24
  1087.9 519.5 %reduce-scatter.3.cloned.1.call-start = ((), (), s32[]{:S(2)}) async-start(), calls=%async_computation.3 | async-start | bytes 17301504 | tf_op jit(solution)/shard_map/while/body/eval_jaxpr/reduce_scatter | solution.py:37
  1476.9 282.9 %all-gather.6.cloned.1.call-start = ((), (), s32[]{:S(2)}) async-start(), calls=%async_computation.4 | async-start | bytes 17301504 | tf_op jit(solution)/shard_map/while/body/eval_jaxpr/all_gather | solution.py:40
  1622.5 432.8 %reduce-scatter.5.cloned.1.call-start = ((), (), s32[]{:S(2)}) async-start(), calls=%async_computation.5 | async-start | bytes 17301504 | tf_op jit(solution)/shard_map/while/body/eval_jaxpr/reduce_scatter | solution.py:43
  1924.7 278.5 %all-gather.8.cloned.1.call-start = ((), (), s32[]{:S(2)}) async-start(), calls=%async_computation.6 | async-start | bytes 17301504 | tf_op jit(solution)/shard_map/while/body/eval_jaxpr/all_gather | solution.py:65
  2065.8 162.8 %copy-start.12 = (f32[1,1408]{1,0:T(1,128)S(1)}, f32[1,1408]{1,0:T(1,128)}, u32[]{:S(2)}) copy-start(f32[1,1408]{1,0:T(1,128)} %get-tuple-element.838) | copy-start | bytes 16900 | tf_op jit(solution)/shard_map/while
  2065.8 162.8 %copy-start.14 = (bf16[1,2816,256]{2,1,0:T(8,128)(2,1)S(1)}, bf16[1,2816,256]{2,1,0:T(8,128)(2,1)}, u32[]{:S(2)}) copy-start(bf16[1,2816,256]{2,1,0:T(8,128)(2,1)} %get-tuple-element.872) | copy-start | bytes 4325380 | tf_op jit(solution)/shard_map/while
  2065.8 162.8 %copy-start.16 = (f32[1,256]{1,0:T(1,128)S(1)}, f32[1,256]{1,0:T(1,128)}, u32[]{:S(2)}) copy-start(f32[1,256]{1,0:T(1,128)} %get-tuple-element.903) | copy-start | bytes 3076 | tf_op jit(solution)/shard_map/while
  2203.2 19.9 collective-permute-start
  2229.1 265.0 %all-gather.4.cloned.1.call-start = ((), (), s32[]{:S(2)}) async-start(), calls=%async_computation.2 | async-start | bytes 17301504 | tf_op jit(solution)/shard_map/while/body/eval_jaxpr/all_gather | solution.py:24
  2248.1 519.5 %reduce-scatter.3.cloned.1.call-start = ((), (), s32[]{:S(2)}) async-start(), calls=%async_computation.3 | async-start | bytes 17301504 | tf_op jit(solution)/shard_map/while/body/eval_jaxpr/reduce_scatter | solution.py:37
  2637.1 282.9 %all-gather.6.cloned.1.call-start = ((), (), s32[]{:S(2)}) async-start(), calls=%async_computation.4 | async-start | bytes 17301504 | tf_op jit(solution)/shard_map/while/body/eval_jaxpr/all_gather | solution.py:40
  2782.6 432.8 %reduce-scatter.5.cloned.1.call-start = ((), (), s32[]{:S(2)}) async-start(), calls=%async_computation.5 | async-start | bytes 17301504 | tf_op jit(solution)/shard_map/while/body/eval_jaxpr/reduce_scatter | solution.py:43
  3084.9 278.5 %all-gather.8.cloned.1.call-start = ((), (), s32[]{:S(2)}) async-start(), calls=%async_computation.6 | async-start | bytes 17301504 | tf_op jit(solution)/shard_map/while/body/eval_jaxpr/all_gather | solution.py:65
  3225.9 162.8 %copy-start.6 = (f32[1,2816]{1,0:T(1,128)S(1)}, f32[1,2816]{1,0:T(1,128)}, u32[]{:S(2)}) copy-start(f32[1,2816]{1,0:T(1,128)} %get-tuple-element.809) | copy-start | bytes 33796 | tf_op jit(solution)/shard_map/while
  3225.9 162.8 %copy-start.12 = (f32[1,1408]{1,0:T(1,128)S(1)}, f32[1,1408]{1,0:T(1,128)}, u32[]{:S(2)}) copy-start(f32[1,1408]{1,0:T(1,128)} %get-tuple-element.838) | copy-start | bytes 16900 | tf_op jit(solution)/shard_map/while
  3225.9 162.8 %copy-start.14 = (bf16[1,2816,256]{2,1,0:T(8,128)(2,1)S(1)}, bf16[1,2816,256]{2,1,0:T(8,128)(2,1)}, u32[]{:S(2)}) copy-start(bf16[1,2816,256]{2,1,0:T(8,128)(2,1)} %get-tuple-element.872) | copy-start | bytes 4325380 | tf_op jit(solution)/shard_map/while
  3225.9 162.8 %copy-start.16 = (f32[1,256]{1,0:T(1,128)S(1)}, f32[1,256]{1,0:T(1,128)}, u32[]{:S(2)}) copy-start(f32[1,256]{1,0:T(1,128)} %get-tuple-element.903) | copy-start | bytes 3076 | tf_op jit(solution)/shard_map/while
  3363.3 19.9 collective-permute-start
  3389.0 265.0 %all-gather.4.cloned.1.call-start = ((), (), s32[]{:S(2)}) async-start(), calls=%async_computation.2 | async-start | bytes 17301504 | tf_op jit(solution)/shard_map/while/body/eval_jaxpr/all_gather | solution.py:24
  3408.0 519.5 %reduce-scatter.3.cloned.1.call-start = ((), (), s32[]{:S(2)}) async-start(), calls=%async_computation.3 | async-start | bytes 17301504 | tf_op jit(solution)/shard_map/while/body/eval_jaxpr/reduce_scatter | solution.py:37
  3797.0 282.9 %all-gather.6.cloned.1.call-start = ((), (), s32[]{:S(2)}) async-start(), calls=%async_computation.4 | async-start | bytes 17301504 | tf_op jit(solution)/shard_map/while/body/eval_jaxpr/all_gather | solution.py:40
  3942.5 432.8 %reduce-scatter.5.cloned.1.call-start = ((), (), s32[]{:S(2)}) async-start(), calls=%async_computation.5 | async-start | bytes 17301504 | tf_op jit(solution)/shard_map/while/body/eval_jaxpr/reduce_scatter | solution.py:43
  4244.8 278.5 %all-gather.8.cloned.1.call-start = ((), (), s32[]{:S(2)}) async-start(), calls=%async_computation.6 | async-start | bytes 17301504 | tf_op jit(solution)/shard_map/while/body/eval_jaxpr/all_gather | solution.py:65
  4385.9 162.8 %copy-start.12 = (f32[1,1408]{1,0:T(1,128)S(1)}, f32[1,1408]{1,0:T(1,128)}, u32[]{:S(2)}) copy-start(f32[1,1408]{1,0:T(1,128)} %get-tuple-element.838) | copy-start | bytes 16900 | tf_op jit(solution)/shard_map/while
  4385.9 162.8 %copy-start.14 = (bf16[1,2816,256]{2,1,0:T(8,128)(2,1)S(1)}, bf16[1,2816,256]{2,1,0:T(8,128)(2,1)}, u32[]{:S(2)}) copy-start(bf16[1,2816,256]{2,1,0:T(8,128)(2,1)} %get-tuple-element.872) | copy-start | bytes 4325380 | tf_op jit(solution)/shard_map/while
  4385.9 162.8 %copy-start.16 = (f32[1,256]{1,0:T(1,128)S(1)}, f32[1,256]{1,0:T(1,128)}, u32[]{:S(2)}) copy-start(f32[1,256]{1,0:T(1,128)} %get-tuple-element.903) | copy-start | bytes 3076 | tf_op jit(solution)/shard_map/while
  4523.3 19.9 collective-permute-start
  4549.1 265.0 %all-gather.4.cloned.1.call-start = ((), (), s32[]{:S(2)}) async-start(), calls=%async_computation.2 | async-start | bytes 17301504 | tf_op jit(solution)/shard_map/while/body/eval_jaxpr/all_gather | solution.py:24
  4568.2 519.5 %reduce-scatter.3.cloned.1.call-start = ((), (), s32[]{:S(2)}) async-start(), calls=%async_computation.3 | async-start | bytes 17301504 | tf_op jit(solution)/shard_map/while/body/eval_jaxpr/reduce_scatter | solution.py:37
  4957.2 282.9 %all-gather.6.cloned.1.call-start = ((), (), s32[]{:S(2)}) async-start(), calls=%async_computation.4 | async-start | bytes 17301504 | tf_op jit(solution)/shard_map/while/body/eval_jaxpr/all_gather | solution.py:40
  5102.7 432.8 %reduce-scatter.5.cloned.1.call-start = ((), (), s32[]{:S(2)}) async-start(), calls=%async_computation.5 | async-start | bytes 17301504 | tf_op jit(solution)/shard_map/while/body/eval_jaxpr/reduce_scatter | solution.py:43
  5404.9 278.5 %all-gather.8.cloned.1.call-start = ((), (), s32[]{:S(2)}) async-start(), calls=%async_computation.6 | async-start | bytes 17301504 | tf_op jit(solution)/shard_map/while/body/eval_jaxpr/all_gather | solution.py:65
  5546.0 162.8 %copy-start.12 = (f32[1,1408]{1,0:T(1,128)S(1)}, f32[1,1408]{1,0:T(1,128)}, u32[]{:S(2)}) copy-start(f32[1,1408]{1,0:T(1,128)} %get-tuple-element.838) | copy-start | bytes 16900 | tf_op jit(solution)/shard_map/while
  5546.0 162.8 %copy-start.14 = (bf16[1,2816,256]{2,1,0:T(8,128)(2,1)S(1)}, bf16[1,2816,256]{2,1,0:T(8,128)(2,1)}, u32[]{:S(2)}) copy-start(bf16[1,2816,256]{2,1,0:T(8,128)(2,1)} %get-tuple-element.872) | copy-start | bytes 4325380 | tf_op jit(solution)/shard_map/while
  5546.0 162.8 %copy-start.16 = (f32[1,256]{1,0:T(1,128)S(1)}, f32[1,256]{1,0:T(1,128)}, u32[]{:S(2)}) copy-start(f32[1,256]{1,0:T(1,128)} %get-tuple-element.903) | copy-start | bytes 3076 | tf_op jit(solution)/shard_map/while
  5683.4 19.9 collective-permute-start
  5709.1 265.0 %all-gather.4.cloned.1.call-start = ((), (), s32[]{:S(2)}) async-start(), calls=%async_computation.2 | async-start | bytes 17301504 | tf_op jit(solution)/shard_map/while/body/eval_jaxpr/all_gather | solution.py:24
  5728.1 519.5 %reduce-scatter.3.cloned.1.call-start = ((), (), s32[]{:S(2)}) async-start(), calls=%async_computation.3 | async-start | bytes 17301504 | tf_op jit(solution)/shard_map/while/body/eval_jaxpr/reduce_scatter | solution.py:37
  6117.1 282.9 %all-gather.6.cloned.1.call-start = ((), (), s32[]{:S(2)}) async-start(), calls=%async_computation.4 | async-start | bytes 17301504 | tf_op jit(solution)/shard_map/while/body/eval_jaxpr/all_gather | solution.py:40
  6262.6 432.8 %reduce-scatter.5.cloned.1.call-start = ((), (), s32[]{:S(2)}) async-start(), calls=%async_computation.5 | async-start | bytes 17301504 | tf_op jit(solution)/shard_map/while/body/eval_jaxpr/reduce_scatter | solution.py:43
  6564.9 278.5 %all-gather.8.cloned.1.call-start = ((), (), s32[]{:S(2)}) async-start(), calls=%async_computation.6 | async-start | bytes 17301504 | tf_op jit(solution)/shard_map/while/body/eval_jaxpr/all_gather | solution.py:65
  6705.9 162.8 %copy-start.12 = (f32[1,1408]{1,0:T(1,128)S(1)}, f32[1,1408]{1,0:T(1,128)}, u32[]{:S(2)}) copy-start(f32[1,1408]{1,0:T(1,128)} %get-tuple-element.838) | copy-start | bytes 16900 | tf_op jit(solution)/shard_map/while
  6705.9 162.8 %copy-start.14 = (bf16[1,2816,256]{2,1,0:T(8,128)(2,1)S(1)}, bf16[1,2816,256]{2,1,0:T(8,128)(2,1)}, u32[]{:S(2)}) copy-start(bf16[1,2816,256]{2,1,0:T(8,128)(2,1)} %get-tuple-element.872) | copy-start | bytes 4325380 | tf_op jit(solution)/shard_map/while
  6705.9 162.8 %copy-start.16 = (f32[1,256]{1,0:T(1,128)S(1)}, f32[1,256]{1,0:T(1,128)}, u32[]{:S(2)}) copy-start(f32[1,256]{1,0:T(1,128)} %get-tuple-element.903) | copy-start | bytes 3076 | tf_op jit(solution)/shard_map/while
  6843.4 19.9 collective-permute-start
  6869.2 265.0 %all-gather.4.cloned.1.call-start = ((), (), s32[]{:S(2)}) async-start(), calls=%async_computation.2 | async-start | bytes 17301504 | tf_op jit(solution)/shard_map/while/body/eval_jaxpr/all_gather | solution.py:24
  6888.2 519.5 %reduce-scatter.3.cloned.1.call-start = ((), (), s32[]{:S(2)}) async-start(), calls=%async_computation.3 | async-start | bytes 17301504 | tf_op jit(solution)/shard_map/while/body/eval_jaxpr/reduce_scatter | solution.py:37
  7277.3 282.9 %all-gather.6.cloned.1.call-start = ((), (), s32[]{:S(2)}) async-start(), calls=%async_computation.4 | async-start | bytes 17301504 | tf_op jit(solution)/shard_map/while/body/eval_jaxpr/all_gather | solution.py:40
  7422.8 432.8 %reduce-scatter.5.cloned.1.call-start = ((), (), s32[]{:S(2)}) async-start(), calls=%async_computation.5 | async-start | bytes 17301504 | tf_op jit(solution)/shard_map/while/body/eval_jaxpr/reduce_scatter | solution.py:43
  7725.0 278.5 %all-gather.8.cloned.1.call-start = ((), (), s32[]{:S(2)}) async-start(), calls=%async_computation.6 | async-start | bytes 17301504 | tf_op jit(solution)/shard_map/while/body/eval_jaxpr/all_gather | solution.py:65
  7866.1 162.8 %copy-start.12 = (f32[1,1408]{1,0:T(1,128)S(1)}, f32[1,1408]{1,0:T(1,128)}, u32[]{:S(2)}) copy-start(f32[1,1408]{1,0:T(1,128)} %get-tuple-element.838) | copy-start | bytes 16900 | tf_op jit(solution)/shard_map/while
  7866.1 162.8 %copy-start.14 = (bf16[1,2816,256]{2,1,0:T(8,128)(2,1)S(1)}, bf16[1,2816,256]{2,1,0:T(8,128)(2,1)}, u32[]{:S(2)}) copy-start(bf16[1,2816,256]{2,1,0:T(8,128)(2,1)} %get-tuple-element.872) | copy-start | bytes 4325380 | tf_op jit(solution)/shard_map/while
  7866.1 162.8 %copy-start.16 = (f32[1,256]{1,0:T(1,128)S(1)}, f32[1,256]{1,0:T(1,128)}, u32[]{:S(2)}) copy-start(f32[1,256]{1,0:T(1,128)} %get-tuple-element.903) | copy-start | bytes 3076 | tf_op jit(solution)/shard_map/while
  8003.5 19.9 collective-permute-start
  (67 other events, 2283.8 us)
Sparse Core Ops, SparseCore 0:
  36.9 136.9 all-gather.3
  317.1 130.3 reduce-scatter.2
  462.7 137.2 all-gather.5
  764.9 130.3 reduce-scatter.4
  906.0 137.2 all-gather.7
  1088.1 245.7 all-gather.3
  1477.0 130.3 reduce-scatter.2
  1622.6 137.2 all-gather.5
  1924.8 130.3 reduce-scatter.4
  2065.9 137.2 all-gather.7
  2248.2 245.7 all-gather.3
  2637.2 130.3 reduce-scatter.2
  2782.7 137.2 all-gather.5
  3085.0 130.3 reduce-scatter.4
  3226.1 137.2 all-gather.7
  3408.1 245.7 all-gather.3
  3797.1 130.3 reduce-scatter.2
  3942.7 137.2 all-gather.5
  4244.9 130.3 reduce-scatter.4
  4386.0 137.2 all-gather.7
  4568.3 245.7 all-gather.3
  4957.3 130.3 reduce-scatter.2
  5102.8 137.2 all-gather.5
  5405.1 130.3 reduce-scatter.4
  5546.2 137.2 all-gather.7
  5728.2 245.7 all-gather.3
  6117.2 130.3 reduce-scatter.2
  6262.7 137.2 all-gather.5
  6565.0 130.3 reduce-scatter.4
  6706.1 137.2 all-gather.7
  6888.4 245.7 all-gather.3
  7277.4 130.3 reduce-scatter.2
  7422.9 137.2 all-gather.5
  7725.1 130.3 reduce-scatter.4
  7866.2 137.2 all-gather.7
where the time goes:
time: 8160 us; the launch traced here: 8060 us
  waiting for transfers between devices  5480 us (67%)
  matrix products  2100 us (26%)
  other arithmetic  311 us (4%)
  local copies, waits for them, and re-layouts  139 us (2%)
    all_gather x7, waiting for transfers between devices, stage_layer(): normed_all = lax.all_gather(normed, 'tp', axis=1, tiled=True)  1610 us
    all_gather x7, waiting for transfers between devices, pipe_step(): gathered = lax.all_gather(stage_out, 'tp', axis=1, tiled=True)  962 us
    all_gather x7, waiting for transfers between devices, stage_layer(): normed2_all = lax.all_gather(normed2, 'tp', axis=1, tiled=True)  961 us
    reduce_scatter x7, waiting for transfers between devices, stage_layer(): mlp_sum = lax.psum_scatter(mlp_part, 'tp', scatter_dimension=1, tiled=True)  909 us
    reduce_scatter x7, waiting for transfers between devices, stage_layer(): lax.psum_scatter(attn_part, 'tp', scatter_dimension=1, tiled=True)  908 us
    dot_general x7, matrix products, stage_layer(): jnp.einsum('bsf,fd->bsd', up_act, w_down, preferred_element_type=jnp.floa...  627 us
    dot_general x7, matrix products, stage_layer(): jnp.einsum('bsd,df->bsf', normed2_all, w_up, preferred_element_type=jnp.f...  526 us
    sub x7, matrix products, stage_layer(): jax.nn.softmax(jnp.where(causal, scores, -1e+30), axis=-1)  311 us
  transfers between devices with their start and end apart: 42, of which 42 were waited for; matrix products, arithmetic and copies ran while one was open for 0% of the time, Pallas kernels for 0%

commit v1 on v0

v1 whole, which is shorter than its diff:
```python
import functools

import jax
import jax.numpy as jnp
from jax import lax
from jax.experimental import pallas as pl
from jax.experimental.pallas import tpu as pltpu
from jax.sharding import PartitionSpec as P

F32 = jnp.float32
BF16 = jnp.bfloat16
MESH = pl.DeviceIdType.MESH

PARAM_SPECS = (P('pp', None), P('pp', None), P('pp', None, 'tp'), P('pp', 'tp'), P('pp', None, None), P('pp', None), P('pp', 'tp', None), P('pp', None), P('pp', None), P('pp', None), P('pp', None, 'tp'), P('pp', 'tp'), P('pp', 'tp', None), P('pp', None))

CW = 256
HEAD = 128
UNIT_ROWS = 256
SLOTS = 8


def stage_kernel(cfg, x_in, g1, s1, wq, bq, wkv, bkv, wo, bo, g2, s2, wup, bup, wdn, bdn,
                 out, x_recv, wq_peer, wo_peer,
                 ring, xbuf, hbuf, qbuf, cbuf, x1own, x1recv, ubuf, zbuf, psend, precv, ybuf, kt, vbuf, bq_all,
                 ring_sem, xload_sem, xrecv_sem, xin_send_sem, w_send_sem, w_recv_sem, x1_send_sem, x1_recv_sem,
                 p_send_sem, p_recv_sem, y_send_sem, out_recv_sem, go_sem):
    (n_stages, n_units, quarters, rows, hidden, ffn_loc) = cfg
    half_q = quarters // 2
    nq = hidden // CW
    nu = ffn_loc // CW
    heads_half = hidden // 2 // HEAD
    n_heads = 2 * heads_half
    scale = HEAD ** -0.5
    stage = lax.axis_index('pp')
    rank = lax.axis_index('tp')
    peer = {'tp': 1 - rank}
    nxt = {'pp': jnp.minimum(stage + 1, n_stages - 1)}
    prv = {'pp': jnp.maximum(stage - 1, 0)}
    first = stage == 0
    last = stage == n_stages - 1
    even = lax.rem(stage, 2) == 0

    counts = (1 + nq, nq, nu, nu, 2 * nq)
    bases = tuple(sum(counts[:i]) for i in range(len(counts)))
    total = sum(counts)

    def slot_of(u, phase, idx):
        return lax.rem(u * total + bases[phase] + idx, SLOTS)

    def start_chunk(u, phase, idx):
        slot = slot_of(u, phase, idx)
        dst = ring.at[slot]
        sem = ring_sem.at[slot]

        def cols(c, width):
            return pl.ds(pl.multiple_of(c * width, width), width)

        if phase == 0:
            @pl.when(idx == 0)
            def _():
                pltpu.make_async_copy(wkv.at[0], dst, sem).start()

            for b in range(2):
                block = (idx - 1) * 2 + b
                piece = dst.at[:, pl.ds(b * HEAD, HEAD)]

                @pl.when((idx > 0) & (block < heads_half))
                def _():
                    pltpu.make_async_copy(wq.at[0, :, cols(block, HEAD)], piece, sem).start()

                @pl.when((idx > 0) & (block >= heads_half))
                def _():
                    pltpu.make_async_copy(wq_peer.at[:, cols(block - heads_half, HEAD)], piece, sem).start()
        elif phase == 1:
            half = hidden // 2
            pltpu.make_async_copy(wo.at[0, :, cols(idx, CW)], dst.at[pl.ds(0, half), :], sem).start()
            pltpu.make_async_copy(wo_peer.at[:, cols(idx, CW)], dst.at[pl.ds(half, half), :], sem).start()
        elif phase in (2, 3):
            pltpu.make_async_copy(wup.at[0, :, cols(idx, CW)], dst, sem).start()
        else:
            part = lax.rem(idx, 2)
            pltpu.make_async_copy(
                wdn.at[0, pl.ds(pl.multiple_of(part * hidden, hidden), hidden), cols(idx // 2, CW)], dst, sem).start()

    def prefetch(u, phase, idx):
        ahead = idx + SLOTS
        n = counts[phase]

        @pl.when(ahead < n)
        def _():
            start_chunk(u, phase, ahead)

        if phase + 1 < len(counts):
            @pl.when(ahead >= n)
            def _():
                start_chunk(u, phase + 1, ahead - n)
        else:
            @pl.when((ahead >= n) & (u + 1 < n_units))
            def _():
                start_chunk(u + 1, 0, ahead - n)

    def wait_chunk(u, phase, idx):
        slot = slot_of(u, phase, idx)
        pltpu.make_async_copy(wkv.at[0], ring.at[slot], ring_sem.at[slot]).wait()
        return slot

    def layer_norm(src, dst, gain, shift):
        block = 32

        def body(i, carry):
            r = pl.ds(pl.multiple_of(i * block, block), block)
            v = src[r, :].astype(F32)
            mean = jnp.mean(v, axis=-1, keepdims=True)
            cen = v - mean
            var = jnp.mean(cen * cen, axis=-1, keepdims=True)
            dst[r, :] = (cen * lax.rsqrt(var + 1e-5) * gain[...] + shift[...]).astype(BF16)
            return carry

        lax.fori_loop(0, rows // block, body, 0)

    def send_x_in(t):
        mb = t // quarters
        j = lax.rem(t, quarters)

        @pl.when(first & (t < n_units) & (j // half_q == rank))
        def _():
            src = x_in.at[mb, 1 - rank, pl.ds(pl.multiple_of(lax.rem(j, half_q) * rows, rows), rows), :]
            pltpu.make_async_remote_copy(src, x_recv.at[t], xin_send_sem.at[t], xrecv_sem.at[t],
                                         device_id=peer, device_id_type=MESH).start()

    def weight_copy(i):
        src, dst = ((bq, bq_all.at[pl.ds(heads_half, heads_half)]), (wq.at[0], wq_peer), (wo.at[0], wo_peer))[i]
        return pltpu.make_async_remote_copy(src, dst, w_send_sem.at[i], w_recv_sem.at[i], device_id=peer, device_id_type=MESH)

    barrier = pltpu.get_barrier_semaphore()
    pl.semaphore_signal(barrier, inc=1, device_id=peer, device_id_type=MESH)

    @pl.when(stage > 0)
    def _():
        pl.semaphore_signal(barrier, inc=1, device_id=prv, device_id_type=MESH)

    @pl.when(jnp.logical_not(last))
    def _():
        pl.semaphore_signal(barrier, inc=1, device_id=nxt, device_id_type=MESH)

    pl.semaphore_wait(barrier, 1 + (stage > 0).astype(jnp.int32) + (stage < n_stages - 1).astype(jnp.int32))

    for t in range(half_q):
        send_x_in(jnp.int32(t))

    @pl.when(jnp.logical_not(even))
    def _():
        pl.semaphore_wait(go_sem, 1)

    for i in range(3):
        weight_copy(i).start()
    bq_all[pl.ds(0, heads_half)] = bq[...]

    own_chunks = 1 + heads_half // 2
    for i in range(min(SLOTS, own_chunks)):
        start_chunk(0, 0, jnp.int32(i))
    weight_copy(0).wait_recv()
    weight_copy(1).wait_recv()
    for i in range(min(SLOTS, own_chunks), SLOTS):
        start_chunk(0, 0, jnp.int32(i))

    def attention(j):
        rh = 128

        def one_head(jj, h):
            q = qbuf[h]
            for b in range(rows // rh):
                nk = rows * jj + rh * (b + 1)
                s = jnp.dot(q[b * rh:(b + 1) * rh], kt[:, :nk], preferred_element_type=F32) * scale
                row = lax.broadcasted_iota(jnp.int32, (rh, nk), 0) + (nk - rh)
                col = lax.broadcasted_iota(jnp.int32, (rh, nk), 1)
                s = jnp.where(col <= row, s, -1e30)
                p = jnp.exp(s - jnp.max(s, axis=-1, keepdims=True))
                p = (p * (1.0 / jnp.sum(p, axis=-1, keepdims=True))).astype(BF16)
                c = jnp.dot(p, vbuf[:nk, :], preferred_element_type=F32)
                cbuf[pl.ds(b * rh, rh), pl.ds(pl.multiple_of(h * HEAD, HEAD), HEAD)] = c.astype(BF16)

        for jj in range(quarters):
            @pl.when(j == jj)
            def _():
                def body(i, carry):
                    one_head(jj, 2 * i)
                    one_head(jj, 2 * i + 1)
                    return carry

                lax.fori_loop(0, n_heads // 2, body, 0)

    def x1_copy(slot, c):
        cols = pl.ds(pl.multiple_of(c * CW, CW), CW)
        return pltpu.make_async_remote_copy(x1own.at[:, cols], x1recv.at[slot, :, cols], x1_send_sem, x1_recv_sem.at[slot],
                                            device_id=peer, device_id_type=MESH)

    def p_copy(slot, c):
        cols = pl.ds(pl.multiple_of(c * CW, CW), CW)
        return pltpu.make_async_remote_copy(psend.at[:, cols], precv.at[slot, :, cols], p_send_sem, p_recv_sem.at[slot],
                                            device_id=peer, device_id_type=MESH)

    def whole(src, dst, send_sem, recv_sem):
        return pltpu.make_async_remote_copy(src, dst, send_sem, recv_sem, device_id=peer, device_id_type=MESH)

    def finish(u):
        slot = lax.rem(u, 2)
        mb = u // quarters
        j = lax.rem(u, quarters)
        whole(psend, precv.at[slot], p_send_sem, p_recv_sem.at[slot]).wait_recv()

        @pl.when(u > 0)
        def _():
            pltpu.make_async_copy(ybuf, x_recv.at[0], y_send_sem).wait()

        block = 32

        def body(i, carry):
            r = pl.ds(pl.multiple_of(i * block, block), block)
            ybuf[r, :] = (zbuf[r, :] + precv[slot, r, :].astype(F32)).astype(BF16)
            return carry

        lax.fori_loop(0, rows // block, body, 0)

        @pl.when(jnp.logical_not(last))
        def _():
            pltpu.make_async_remote_copy(ybuf, x_recv.at[u], y_send_sem, xrecv_sem.at[u], device_id=nxt, device_id_type=MESH).start()

        place = out.at[mb, rank, pl.ds(pl.multiple_of(lax.rem(j, half_q) * rows, rows), rows), :]

        @pl.when(last & (j // half_q == rank))
        def _():
            pltpu.make_async_copy(ybuf, place, y_send_sem).start()

        @pl.when(last & (j // half_q != rank))
        def _():
            pltpu.make_async_remote_copy(ybuf, place, y_send_sem, out_recv_sem.at[u], device_id=peer, device_id_type=MESH).start()

    def up(u, phase, row0):
        def body(c, carry):
            slot = wait_chunk(u, phase, c)
            a = jnp.dot(hbuf[...], ring[slot], preferred_element_type=F32) + bup[c]
            t = jnp.tanh(0.7978845608028654 * (a + 0.044715 * (a * a * a)))
            ubuf[pl.ds(row0, rows), pl.ds(pl.multiple_of(c * CW, CW), CW)] = (0.5 * a * (1.0 + t)).astype(BF16)
            prefetch(u, phase, c)
            return carry

        lax.fori_loop(0, nu, body, 0)

    def unit(u, carry):
        mb = u // quarters
        j = lax.rem(u, quarters)
        slot2 = lax.rem(u, 2)

        send_x_in(u + half_q)
        local = first & (j // half_q == rank)

        @pl.when(local)
        def _():
            src = x_in.at[mb, rank, pl.ds(pl.multiple_of(lax.rem(j, half_q) * rows, rows), rows), :]
            pltpu.make_async_copy(src, xbuf, xload_sem).start()

        @pl.when(jnp.logical_not(local))
        def _():
            pltpu.make_async_remote_copy(ybuf, x_recv.at[u], y_send_sem, xrecv_sem.at[u], device_id=peer, device_id_type=MESH).wait_recv()
            pltpu.make_async_copy(x_recv.at[u], xbuf, xload_sem).start()

        pltpu.make_async_copy(x_recv.at[0], xbuf, xload_sem).wait()
        layer_norm(xbuf, hbuf, g1, s1)

        slot = wait_chunk(u, 0, 0)
        kv = jnp.dot(hbuf[...], ring[slot], preferred_element_type=F32) + bkv[...]
        at = pl.ds(pl.multiple_of(j * rows, rows), rows)
        kt[:, at] = kv[:, :HEAD].astype(BF16).astype(F32).T.astype(BF16)
        vbuf[at, :] = kv[:, HEAD:].astype(BF16)
        prefetch(u, 0, 0)

        @pl.when(u == 0)
        def _():
            weight_copy(2).wait_recv()
            for i in range(3):
                weight_copy(i).wait_send()

            @pl.when(even)
            def _():
                pl.semaphore_signal(go_sem, inc=1, device_id=nxt, device_id_type=MESH)

        def q_body(c, carry):
            slot = wait_chunk(u, 0, c + 1)
            a = jnp.dot(hbuf[...], ring[slot], preferred_element_type=F32)
            qbuf[2 * c] = (a[:, :HEAD] + bq_all[2 * c]).astype(BF16)
            qbuf[2 * c + 1] = (a[:, HEAD:] + bq_all[2 * c + 1]).astype(BF16)
            prefetch(u, 0, c + 1)
            return carry

        lax.fori_loop(0, nq, q_body, 0)
        attention(j)

        @pl.when(u > 0)
        def _():
            whole(x1own, x1recv.at[slot2], x1_send_sem, x1_recv_sem.at[slot2]).wait_send()

        def o_body(c, carry):
            slot = wait_chunk(u, 1, c)
            cols = pl.ds(pl.multiple_of(c * CW, CW), CW)
            a = jnp.dot(cbuf[...], ring[slot], preferred_element_type=F32)
            x1own[:, cols] = (xbuf[:, cols].astype(F32) + a + bo[c]).astype(BF16)

            @pl.when(c > 0)
            def _():
                x1_copy(slot2, c - 1).start()

            prefetch(u, 1, c)
            return carry

        lax.fori_loop(0, nq, o_body, 0)
        layer_norm(x1own, hbuf, g2, s2)
        x1_copy(slot2, nq - 1).start()

        up(u, 2, 0)

        @pl.when(u > 0)
        def _():
            finish(u - 1)

        whole(x1own, x1recv.at[slot2], x1_send_sem, x1_recv_sem.at[slot2]).wait_recv()
        layer_norm(x1recv.at[slot2], hbuf, g2, s2)
        up(u, 3, rows)

        @pl.when(u > 0)
        def _():
            whole(psend, precv.at[slot2], p_send_sem, p_recv_sem.at[slot2]).wait_send()

        def down_body(c, carry):
            cols = pl.ds(pl.multiple_of(c * CW, CW), CW)
            slot_a = wait_chunk(u, 4, 2 * c)
            slot_b = wait_chunk(u, 4, 2 * c + 1)
            a = (jnp.dot(ubuf[:, :hidden], ring[slot_a], preferred_element_type=F32)
                 + jnp.dot(ubuf[:, hidden:], ring[slot_b], preferred_element_type=F32))
            zbuf[:, cols] = x1own[:, cols].astype(F32) + a[:rows] + bdn[c]
            psend[:, cols] = a[rows:].astype(BF16)

            @pl.when(c > 0)
            def _():
                p_copy(slot2, c - 1).start()

            prefetch(u, 4, 2 * c)
            prefetch(u, 4, 2 * c + 1)
            return carry

        lax.fori_loop(0, nq, down_body, 0)
        p_copy(slot2, nq - 1).start()
        return carry

    lax.fori_loop(0, n_units, unit, 0)
    end = n_units - 1
    finish(jnp.int32(end))

    whole(x1own, x1recv.at[end % 2], x1_send_sem, x1_recv_sem.at[end % 2]).wait_send()
    whole(psend, precv.at[end % 2], p_send_sem, p_recv_sem.at[end % 2]).wait_send()
    pltpu.make_async_copy(ybuf, x_recv.at[0], y_send_sem).wait()

    def drain(t, carry):
        j = lax.rem(t, quarters)
        mine = j // half_q == rank

        @pl.when(first & mine)
        def _():
            pltpu.make_async_remote_copy(ybuf, x_recv.at[t], xin_send_sem.at[t], xrecv_sem.at[t], device_id=peer, device_id_type=MESH).wait_send()

        @pl.when(last & mine)
        def _():
            place = out.at[t // quarters, 1 - rank, pl.ds(pl.multiple_of(lax.rem(j, half_q) * rows, rows), rows), :]
            pltpu.make_async_remote_copy(ybuf, place, y_send_sem, out_recv_sem.at[t], device_id=peer, device_id_type=MESH).wait_recv()

        return carry

    lax.fori_loop(0, n_units, drain, 0)


def run_stage(x_loc, params, n_stages):
    (ln1_gain, ln1_bias, w_q, b_q, w_kv, b_kv, w_o, b_o, ln2_gain, ln2_bias, w_up, b_up, w_down, b_down) = params
    n_micro, _, seq_loc, hidden = x_loc.shape
    ffn_loc = w_up.shape[2]
    rows = min(UNIT_ROWS, seq_loc // 2)
    quarters = 2 * seq_loc // rows
    n_units = n_micro * quarters
    nq = hidden // CW
    nu = ffn_loc // CW
    heads_half = hidden // 2 // HEAD
    cfg = (n_stages, n_units, quarters, rows, hidden, ffn_loc)
    vmem = pl.BlockSpec(memory_space=pltpu.VMEM)
    anym = pl.BlockSpec(memory_space=pl.ANY)
    args = (
        x_loc, ln1_gain, ln1_bias, w_q, b_q.reshape(heads_half, 1, HEAD), w_kv, b_kv, w_o, b_o.reshape(nq, 1, CW),
        ln2_gain, ln2_bias, w_up, b_up.reshape(nu, 1, CW), w_down, b_down.reshape(nq, 1, CW),
    )
    in_specs = [anym, vmem, vmem, anym, vmem, anym, vmem, anym, vmem, vmem, vmem, anym, vmem, anym, vmem]
    out_shape = (
        jax.ShapeDtypeStruct(x_loc.shape, BF16),
        jax.ShapeDtypeStruct((n_units, rows, hidden), BF16),
        jax.ShapeDtypeStruct((hidden, hidden // 2), BF16),
        jax.ShapeDtypeStruct((hidden // 2, hidden), BF16),
    )
    dma = pltpu.SemaphoreType.DMA
    scratch = [
        pltpu.VMEM((SLOTS, hidden, CW), BF16),
        pltpu.VMEM((rows, hidden), BF16),
        pltpu.VMEM((rows, hidden), BF16),
        pltpu.VMEM((2 * heads_half, rows, HEAD), BF16),
        pltpu.VMEM((rows, hidden), BF16),
        pltpu.VMEM((rows, hidden), BF16),
        pltpu.VMEM((2, rows, hidden), BF16),
        pltpu.VMEM((2 * rows, ffn_loc), BF16),
        pltpu.VMEM((rows, hidden), F32),
        pltpu.VMEM((rows, hidden), BF16),
        pltpu.VMEM((2, rows, hidden), BF16),
        pltpu.VMEM((rows, hidden), BF16),
        pltpu.VMEM((HEAD, quarters * rows), BF16),
        pltpu.VMEM((quarters * rows, HEAD), BF16),
        pltpu.VMEM((2 * heads_half, 1, HEAD), F32),
        dma((SLOTS,)),
        dma,
        dma((n_units,)),
        dma((n_units,)),
        dma((3,)),
        dma((3,)),
        dma,
        dma((2,)),
        dma,
        dma((2,)),
        dma,
        dma((n_units,)),
        pltpu.SemaphoreType.REGULAR,
    ]
    return pl.pallas_call(
        functools.partial(stage_kernel, cfg),
        out_shape=out_shape,
        in_specs=in_specs,
        out_specs=(anym,) * 4,
        scratch_shapes=scratch,
        compiler_params=pltpu.CompilerParams(collective_id=0, has_side_effects=True, vmem_limit_bytes=60 * 2 ** 20),
        name='stage_loop',
    )(*args)[0]


def solution(mesh):
    pp_size = mesh.shape['pp']

    def stage_program(x_loc, *params):
        result = run_stage(x_loc, params, pp_size)
        is_last = lax.axis_index('pp') == pp_size - 1
        return jnp.where(is_last, result, jnp.zeros_like(result))[None]

    return jax.shard_map(stage_program, mesh=mesh, in_specs=(P(None, 'dp', 'tp', None),) + PARAM_SPECS, out_specs=P('pp', None, 'dp', 'tp', None), check_vma=False)
```

time: 8160 us -> 2250 us (0.28); the launches traced: 8060 us -> 2250 us
  waiting for transfers between devices: 5480 us -> 0 us
  Pallas kernels: 0 us -> 2230 us
  matrix products: 2100 us -> 0 us
  other arithmetic: 311 us -> 19.9 us
  local copies, waits for them, and re-layouts: 139 us -> 0 us
    all_gather x21 -> x0, waiting for transfers between devices: 3530 us -> none  [the longest x7 1610 us: stage_layer(): normed_all = lax.all_gather(normed, 'tp', axis=1, tiled=True)]
    pallas_call x0 -> x1, Pallas kernels: none -> 2230 us  [run_stage(): pl.pallas_call(functools.partial(stage_kernel, cfg), out_shape=out_shape,...]
    reduce_scatter x14 -> x0, waiting for transfers between devices: 1820 us -> none  [the longest x7 909 us: stage_layer(): mlp_sum = lax.psum_scatter(mlp_part, 'tp', scatter_dimension=1, tiled=True)]
    dot_general x42 -> x0, matrix products: 1790 us -> none  [the longest x7 627 us: stage_layer(): jnp.einsum('bsf,fd->bsd', up_act, w_down, preferred_element_type=jnp.floa...]
    sub x7 -> x0, matrix products: 311 us -> none  [stage_layer(): jax.nn.softmax(jnp.where(causal, scores, -1e+30), axis=-1)]
    ppermute x7 -> x0, waiting for transfers between devices: 130 us -> none  [pipe_step(): handed_on = lax.ppermute(gathered, 'pp', send_pairs)]
    reduce_sum x28 -> x0, other arithmetic: 116 us -> none  [the longest x14 92.7 us: layer_norm(): average = jnp.mean(values, axis=-1, keepdims=True)]
    convert_element_type x14 -> x0, other arithmetic: 97.5 us -> none  [the longest x7 57.4 us: stage_layer(): normed = layer_norm(residual, ln1_gain, ln1_bias).astype(jnp.bfloat16)]
  transfers between devices with their start and end apart: 42 -> 0, of which waited for: 42 -> 0; matrix products, arithmetic and copies ran while one was open for 0% -> 0% of each run, Pallas kernels for 0% -> 0%
where the time goes in v1:
time: 2250 us
  Pallas kernels  2230 us (99%)
    pallas_call x1, Pallas kernels, run_stage(): pl.pallas_call(functools.partial(stage_kernel, cfg), out_shape=out_shape,...  2230 us

profile of v1, /device:TPU:7, one launch (start us, length us, event | category | flops | bytes accessed | tf_op | source)
XLA Modules:
  0.0 2252.6 jit_solution(5718106210074412761)
XLA Ops:
  0.0 2232.7 %stage_loop.1 = (bf16[4,2,512,2816]{3,2,1,0:T(8,128)(2,1)}, bf16[16,256,2816]{2,1,0:T(8,128)(2,1)}, bf16[2816,1408]{1,0:T(8,128)(2,1)}, bf16[1408,2816]{1,0:T(8,128)(2,1)}) custom-call(bf16[4,2,512,2816]{3,2,1,0:T(8,128)(2,1)} %x_in.1, f32[1,2816]{1,0:T(1,128)} %g1.1, f32[1,2816]{1,0:T(1,128)} %s1_.1, bf16[1,2816,1408]{2,1,0:T(8,128)(2,1)} %wq.1, ...), custom_call_target="tpu_custom_call" | custom-call | tf_op jit(solution)/shard_map/stage_loop/pallas_call | solution.py:436
  2232.7 19.9 select_bitcast_fusion
